TPU v7x, 32 devices: a whole 2x2x4 slice. The times are simulated.
32 devices in a mesh: dp: 8 (over z, x), mp: 4 (over y, core).
Axes of the slice: x: 2, y: 2, z: 4, core: 2. Of those that a mesh axis runs over, the one named last changes fastest.
Arguments:
- tokens: bfloat16 [1024, 4096], P('dp'), may hold values from -6 to 6
- cotangent: bfloat16 [1024, 4096], P('dp', 'mp'), may hold values from -6 to 6
- sketch: float32 [4096, 128], P('dp'), may hold values from -12 to 12
Outputs:
- precond: bfloat16 [4096, 4096], P('dp', 'mp')
- new_sketch: float32 [4096, 128], P('dp')
All inputs are finite; a program needn't handle non-finite values.
Results may differ from a plain program's by a relative error of at most 0.001.
Values sent between devices are 32-bit elements; how exact they have to be, the bound alone decides.
A program may use at most 64 MiB of HBM per device.

v0:
```python
import functools
import math

import jax
import jax.numpy as jnp
from jax import lax
from jax.experimental import pallas as pl
from jax.experimental.pallas import tpu as pltpu
from jax.sharding import PartitionSpec as P

DECAY_RATE = 0.9
RIDGE_FRAC = 0.0001
MESH = pl.DeviceIdType.MESH
VMEM = pltpu.MemorySpace.VMEM
VMEM_BUDGET = 48 * 2**20


def product(left_mat, right_mat, dims=((1,), (0,))):
    return lax.dot_general(
        left_mat,
        right_mat,
        (dims, ((), ())),
        precision=lax.Precision.HIGHEST,
        preferred_element_type=jnp.float32,
    )


TN = ((0,), (0,))
NT = ((1,), (1,))


def remote(src, dst, send, recv, where):
    return pltpu.make_async_remote_copy(
        src_ref=src,
        dst_ref=dst,
        send_sem=send,
        recv_sem=recv,
        device_id=where,
        device_id_type=MESH,
    )


def inverse_factor(matrix):
    n = matrix.shape[0]
    start = jnp.where(
        lax.broadcasted_iota(jnp.int32, (n, n), 0) == lax.broadcasted_iota(jnp.int32, (n, n), 1), 1.0, 0.0
    ).astype(jnp.float32)
    left = [matrix[8 * i : 8 * i + 8] for i in range(n // 8)]
    right = [start[8 * i : 8 * i + 8] for i in range(n // 8)]
    row_of = lax.broadcasted_iota(jnp.int32, (8, 1), 0)
    rows = []
    for j in range(0, n, 2):
        t, s = divmod(j, 8)
        a0, a1 = left[t][s : s + 1], left[t][s + 1 : s + 2]
        b0, b1 = right[t][s : s + 1], right[t][s + 1 : s + 2]
        pivot, side, corner = a0[:, j : j + 1], a0[:, j + 1 : j + 2], a1[:, j + 1 : j + 2]
        inv0 = 1.0 / pivot
        factor = side * inv0
        a1, b1 = a1 - factor * a0, b1 - factor * b0
        second = corner - factor * side
        inv1 = 1.0 / second
        rows += [b0 * lax.rsqrt(pivot), b1 * lax.rsqrt(second)]
        a0, b0, a1, b1 = a0 * inv0, b0 * inv0, a1 * inv1, b1 * inv1
        for i in range(t, n // 8):
            c0, c1 = left[i][:, j : j + 1], left[i][:, j + 1 : j + 2]
            c1 = c1 - factor * c0
            if i == t:
                c0 = jnp.where(row_of > s + 1, c0, 0.0)
                c1 = jnp.where(row_of > s + 1, c1, 0.0)
            left[i] = left[i] - c0 * a0 - c1 * a1
            right[i] = right[i] - c0 * b0 - c1 * b1
    return jnp.concatenate(rows, axis=0)


def factor_kernel(matrix_ref, inverse_ref):
    inverse_ref[...] = inverse_factor(matrix_ref[...])


def finish_kernel(low_ref, cross_ref, self_ref, new_ref, mixer_ref):
    rank_size = low_ref.shape[0]
    half = product(low_ref[...], cross_ref[...])
    rayleigh = 0.5 * (half + half.T)
    square = (rank_size, rank_size)
    diagonal = lax.broadcasted_iota(jnp.int32, square, 0) == lax.broadcasted_iota(jnp.int32, square, 1)
    mean_level = jnp.sum(jnp.where(diagonal, rayleigh, 0.0)) / rank_size
    shifted = rayleigh + jnp.where(diagonal, RIDGE_FRAC * mean_level, 0.0)
    new_inv = inverse_factor(shifted)
    new_ref[...] = new_inv
    self_gram = product(product(new_inv, self_ref[...]), new_inv, NT)
    inner_inv = inverse_factor(self_gram + jnp.where(diagonal, mean_level, 0.0))
    mixer_ref[...] = product(inner_inv.T, product(inner_inv, new_inv))


def small_call(kernel, count, name, *arrays):
    shape = jax.ShapeDtypeStruct(arrays[0].shape, jnp.float32)
    return pl.pallas_call(
        kernel,
        out_shape=(shape,) * count,
        in_specs=[pl.BlockSpec(memory_space=VMEM)] * len(arrays),
        out_specs=(pl.BlockSpec(memory_space=VMEM),) * count,
        name=name,
    )(*arrays)


def reduce_kernel(axis, n, with_factor, *refs):
    if with_factor:
        x_ref, matrix_ref, o_ref, inverse_ref, *refs = refs
    else:
        x_ref, o_ref, *refs = refs
    land, own, send_a, recv_a, send_b, recv_b = refs
    me = lax.axis_index(axis)
    chunk = own.shape[0]
    barrier = pltpu.get_barrier_semaphore()
    peers = [lax.rem(me + k, n) for k in range(1, n)]
    for peer in peers:
        pl.semaphore_signal(barrier, inc=1, device_id={axis: peer}, device_id_type=MESH)
    pl.semaphore_wait(barrier, n - 1)
    scatter = [
        remote(
            x_ref.at[pl.ds(pl.multiple_of(peer * chunk, 8), chunk)],
            land.at[k],
            send_a.at[k],
            recv_a.at[k],
            {axis: peer},
        )
        for k, peer in enumerate(peers)
    ]
    for copy in scatter:
        copy.start()
    if with_factor:
        inverse_ref[...] = inverse_factor(matrix_ref[...])
    mine = pl.ds(pl.multiple_of(me * chunk, 8), chunk)
    total = x_ref[mine]
    for k, copy in enumerate(scatter):
        copy.wait_recv()
        total = total + land[k]
    own[...] = total
    gather = [
        remote(own, o_ref.at[mine], send_b.at[k], recv_b.at[k], {axis: peer})
        for k, peer in enumerate(peers)
    ]
    for copy in gather:
        copy.start()
    o_ref[mine] = total
    for copy in scatter:
        copy.wait_send()
    for copy in gather:
        copy.wait()


def all_sum(arrays, axis, ident, matrix=None):
    n = lax.axis_size(axis)
    rows = sum(a.shape[0] for a in arrays)
    if rows % (8 * n) or n > 16:
        summed = lax.psum(tuple(arrays), axis)
        return summed if matrix is None else summed + small_call(factor_kernel, 1, "factor", matrix)
    joined = arrays[0] if len(arrays) == 1 else jnp.concatenate(arrays, axis=0)
    width = joined.shape[1]
    chunk = rows // n
    operands = (joined,) if matrix is None else (joined, matrix)
    summed, *inverse = pl.pallas_call(
        functools.partial(reduce_kernel, axis, n, matrix is not None),
        out_shape=tuple(jax.ShapeDtypeStruct(a.shape, jnp.float32) for a in operands),
        in_specs=[pl.BlockSpec(memory_space=VMEM)] * len(operands),
        out_specs=(pl.BlockSpec(memory_space=VMEM),) * len(operands),
        scratch_shapes=[
            pltpu.VMEM((n - 1, chunk, width), jnp.float32),
            pltpu.VMEM((chunk, width), jnp.float32),
        ]
        + [pltpu.SemaphoreType.DMA((n - 1,))] * 4,
        compiler_params=pltpu.CompilerParams(collective_id=ident, has_side_effects=True),
        name=f"sum_{axis}_{ident}",
    )(*operands)
    outs, at = [], 0
    for a in arrays:
        outs.append(summed[at : at + a.shape[0]])
        at += a.shape[0]
    return tuple(outs + inverse)


def gradient_kernel(
    nd, nm, pieces, scale, x_ref, y_ref, g_ref, xland, yland, xt, yb,
    local, xs, xr, ms, mr, zs, zr, fs, fr, os, orr,
):
    d, m = lax.axis_index("dp"), lax.axis_index("mp")
    rows, block = xland.shape[1], xland.shape[2]
    share = rows // nm
    nz = nd // 2
    z, x = lax.div(d, 2), lax.rem(d, 2)
    other = 2 * z + 1 - x
    barrier = pltpu.get_barrier_semaphore()
    for k in range(1, nd):
        pl.semaphore_signal(barrier, inc=1, device_id={"dp": lax.rem(d + k, nd)}, device_id_type=MESH)
    for k in range(1, nm):
        pl.semaphore_signal(barrier, inc=1, device_id={"mp": lax.rem(m + k, nm)}, device_id_type=MESH)
    pl.semaphore_wait(barrier, nd + nm - 2)

    part = pl.ds(pl.multiple_of(m * share, 8), share)
    x_out = []
    for k in range(1, nd):
        peer = lax.rem(d + k, nd)
        cols = pl.ds(pl.multiple_of(peer * block, 128), block)
        x_out.append(
            remote(x_ref.at[part, cols], xland.at[d, part], xs.at[k - 1], xr.at[k - 1], {"dp": peer})
        )
    piece = rows // pieces
    cuts = [pl.ds(c * piece, piece) for c in range(pieces)]

    def along(way, k, c):
        source = 2 * (z - way * k) + x
        at = yland.at[source, cuts[c]]
        return remote(
            y_ref.at[cuts[c]] if k == 0 else at,
            at,
            zs.at[(way + 1) // 2, k, c],
            zr.at[(way + 1) // 2, k, c],
            {"dp": 2 * (z + way) + x},
        )

    def across(way, k, c):
        at = yland.at[2 * (z - way * (k + 1)) + x, cuts[c]]
        return remote(at, at, fs.at[(way + 1) // 2, k, c], fr.at[(way + 1) // 2, k, c], {"dp": other})

    def inside(place):
        return jnp.logical_and(place >= 0, place < nz)

    def sends(way, k):
        return jnp.logical_and(inside(z - way * k), inside(z + way))

    def streams(steps):
        return [(way, k, c) for k in range(steps) for c in range(pieces) for way in (1, -1)]

    over = [
        remote(y_ref.at[cut], yland.at[d, cut], os.at[c], orr.at[c], {"dp": other})
        for c, cut in enumerate(cuts)
    ]
    for c in range(pieces):
        for way in (1, -1):
            pl.when(sends(way, 0))(lambda way=way, c=c: along(way, 0, c).start())
        over[c].start()
        if c == 0:
            for copy in x_out:
                copy.start()
    mine = pl.ds(pl.multiple_of(d * block, 128), block)
    keep_x = pltpu.make_async_copy(x_ref.at[:, mine], xland.at[d], local.at[0])
    keep_y = pltpu.make_async_copy(y_ref, yland.at[d], local.at[1])
    keep_x.start()
    keep_y.start()

    passed = []
    for k in range(1, nd):
        x_out[k - 1].wait_recv()
        source = lax.rem(d + nd - k, nd)
        for j in range(1, nm):
            copy = remote(
                xland.at[source, part],
                xland.at[source, part],
                ms.at[k - 1, j - 1],
                mr.at[k - 1, j - 1],
                {"mp": lax.rem(m + j, nm)},
            )
            copy.start()
            passed.append(copy)
    for way, k, c in streams(nz - 1):

        @pl.when(inside(z - way * (k + 1)))
        def _():
            along(way, k, c).wait_recv()
            across(way, k, c).start()

            if k + 1 < nz - 1:

                @pl.when(inside(z + way))
                def _():
                    along(way, k + 1, c).start()

    keep_x.wait()
    keep_y.wait()
    for copy in passed:
        copy.wait_recv()
    for s in range(nd):
        xt[:, s * rows : (s + 1) * rows] = xland[s].T.astype(jnp.bfloat16)
    for copy in over:
        copy.wait_recv()
    for way, k, c in streams(nz - 1):
        pl.when(inside(z - way * (k + 1)))(lambda way=way, k=k, c=c: across(way, k, c).wait())
    for s in range(nd):
        yb[s * rows : (s + 1) * rows, :] = yland[s].astype(jnp.bfloat16)
    width = yb.shape[1]
    tile = 256 if width % 256 == 0 else width

    def body(t, carry):
        cols = pl.ds(pl.multiple_of(t * tile, 128), tile)
        g_ref[:, cols] = scale * jnp.dot(xt[...], yb[:, cols], preferred_element_type=jnp.float32)
        return carry

    lax.fori_loop(0, width // tile, body, 0)
    for copy in x_out + passed + over:
        copy.wait_send()
    for way, k, c in streams(nz - 1):
        pl.when(sends(way, k))(lambda way=way, k=k, c=c: along(way, k, c).wait_send())


def gradient_block(tokens, cotangent, norm_scale):
    nd, nm = lax.axis_size("dp"), lax.axis_size("mp")
    rows, depth = tokens.shape
    width = cotangent.shape[1]
    block = depth // nd
    need = 4 * rows * (depth + width) + 6 * nd * rows * (block + width) + 4 * block * width
    if need > VMEM_BUDGET or nd % 2 or rows % (8 * nm) or block % 128 or width % 128:
        partial = lax.dot_general(
            tokens, cotangent, (((0,), (0,)), ((), ())), preferred_element_type=jnp.float32
        )
        return lax.psum_scatter(partial * norm_scale, "dp", scatter_dimension=0, tiled=True)
    nz = nd // 2
    pieces = 2 if rows % 16 == 0 else 1
    dma = pltpu.SemaphoreType.DMA
    return pl.pallas_call(
        functools.partial(gradient_kernel, nd, nm, pieces, norm_scale),
        out_shape=jax.ShapeDtypeStruct((block, width), jnp.float32),
        in_specs=[pl.BlockSpec(memory_space=VMEM)] * 2,
        out_specs=pl.BlockSpec(memory_space=VMEM),
        scratch_shapes=[
            pltpu.VMEM((nd, rows, block), jnp.float32),
            pltpu.VMEM((nd, rows, width), jnp.float32),
            pltpu.VMEM((block, nd * rows), jnp.bfloat16),
            pltpu.VMEM((nd * rows, width), jnp.bfloat16),
            dma((2,)),
            dma((nd - 1,)),
            dma((nd - 1,)),
            dma((nd - 1, nm - 1)),
            dma((nd - 1, nm - 1)),
            dma((2, nz - 1, pieces)),
            dma((2, nz - 1, pieces)),
            dma((2, nz - 1, pieces)),
            dma((2, nz - 1, pieces)),
            dma((pieces,)),
            dma((pieces,)),
        ],
        compiler_params=pltpu.CompilerParams(
            collective_id=0, has_side_effects=True, vmem_limit_bytes=60 * 2**20
        ),
        name="gradient_block",
    )(tokens.astype(jnp.float32), cotangent.astype(jnp.float32))


def halves(value, axis):
    high = value.astype(jnp.bfloat16)
    low = (value - high.astype(jnp.float32)).astype(jnp.bfloat16)
    return jnp.concatenate([high, low], axis=axis)


def folded(value, axis):
    n = value.shape[axis] // 2
    if axis == 0:
        return value[:n] + value[n:]
    return value[:, :n] + value[:, n:]


def exact_left(left, right):
    return folded(jnp.dot(left, halves(right, 1), preferred_element_type=jnp.float32), 1)


def exact_right(left, right):
    return folded(jnp.dot(halves(left, 0), right, preferred_element_type=jnp.float32), 0)


def times(left, right):
    both = halves(right, 1)
    full = jnp.concatenate([both, both], axis=0)
    return folded(jnp.dot(halves(left, 1), full, preferred_element_type=jnp.float32), 1)


def gram(left, right):
    full = jnp.dot(halves(left.T, 0), halves(right, 1), preferred_element_type=jnp.float32)
    return folded(folded(full, 0), 1)


def factor_steps(matrix, result):
    n = matrix.shape[0]
    start = jnp.where(
        lax.broadcasted_iota(jnp.int32, (n, n), 0) == lax.broadcasted_iota(jnp.int32, (n, n), 1), 1.0, 0.0
    ).astype(jnp.float32)
    left = [matrix[8 * i : 8 * i + 8] for i in range(n // 8)]
    right = [start[8 * i : 8 * i + 8] for i in range(n // 8)]
    row_of = lax.broadcasted_iota(jnp.int32, (8, 1), 0)
    rows = []
    for j in range(0, n, 2):
        t, s = divmod(j, 8)
        a0, a1 = left[t][s : s + 1], left[t][s + 1 : s + 2]
        b0, b1 = right[t][s : s + 1], right[t][s + 1 : s + 2]
        pivot, side, corner = a0[:, j : j + 1], a0[:, j + 1 : j + 2], a1[:, j + 1 : j + 2]
        inv0 = 1.0 / pivot
        factor = side * inv0
        a1, b1 = a1 - factor * a0, b1 - factor * b0
        second = corner - factor * side
        inv1 = 1.0 / second
        rows += [b0 * lax.rsqrt(pivot), b1 * lax.rsqrt(second)]
        a0, b0, a1, b1 = a0 * inv0, b0 * inv0, a1 * inv1, b1 * inv1
        for i in range(t, n // 8):
            c0, c1 = left[i][:, j : j + 1], left[i][:, j + 1 : j + 2]
            c1 = c1 - factor * c0
            if i == t:
                c0 = jnp.where(row_of > s + 1, c0, 0.0)
                c1 = jnp.where(row_of > s + 1, c1, 0.0)
            left[i] = left[i] - c0 * a0 - c1 * a1
            right[i] = right[i] - c0 * b0 - c1 * b1
        if s == 6:
            yield
    result.append(jnp.concatenate(rows, axis=0))


def run_with(steps, actions):
    actions = list(actions)
    for _ in steps:
        if actions:
            actions.pop(0)()
    for action in actions:
        action()


def whole_kernel(nd, nm, pieces, scale, tok_ref, cot_ref, s_ref, pre_ref, new_ref, *refs):
    (
        xf, yf, xland, yland, xt, xb, yb, g, upart, uland, uown, u, kept, ssf,
        ppart, pland, psum, pother, w,
        local, xs, xr, ms, mr, zs, zr, fs, fr, os, orr,
        us, ur, gs, gr, ss, sr, ys, yr, cs, cr, ks, kr,
        ps, pr, qs, qr, ts, tr,
    ) = refs
    d, m = lax.axis_index("dp"), lax.axis_index("mp")
    rows, block = xland.shape[1], xland.shape[2]
    width = yb.shape[1]
    rank = s_ref.shape[1]
    share = rows // nm
    count = nd * rows
    quarter = count // nm
    slab = rank // nd
    nz = nd // 2
    z, x = lax.div(d, 2), lax.rem(d, 2)
    other = 2 * z + 1 - x
    my, mc = lax.div(m, 2), lax.rem(m, 2)
    mate = 2 * my + 1 - mc
    facing = 2 * (1 - my) + mc
    barrier = pltpu.get_barrier_semaphore()
    for k in range(1, nd):
        pl.semaphore_signal(barrier, inc=1, device_id={"dp": lax.rem(d + k, nd)}, device_id_type=MESH)
    for k in range(1, nm):
        pl.semaphore_signal(barrier, inc=1, device_id={"mp": lax.rem(m + k, nm)}, device_id_type=MESH)
    yf[...] = cot_ref[...].astype(jnp.float32)
    xf[...] = tok_ref[...].astype(jnp.float32)
    pl.semaphore_wait(barrier, nd + nm - 2)

    part = pl.ds(pl.multiple_of(m * share, 8), share)
    x_out = []
    for k in range(1, nd):
        peer = lax.rem(d + k, nd)
        cols = pl.ds(pl.multiple_of(peer * block, 128), block)
        x_out.append(remote(xf.at[part, cols], xland.at[d, part], xs.at[k - 1], xr.at[k - 1], {"dp": peer}))
    piece = rows // pieces
    cuts = [pl.ds(c * piece, piece) for c in range(pieces)]

    def along(way, k, c):
        source = 2 * (z - way * k) + x
        at = yland.at[source, cuts[c]]
        return remote(
            yf.at[cuts[c]] if k == 0 else at,
            at,
            zs.at[(way + 1) // 2, k, c],
            zr.at[(way + 1) // 2, k, c],
            {"dp": 2 * (z + way) + x},
        )

    def across(way, k, c):
        at = yland.at[2 * (z - way * (k + 1)) + x, cuts[c]]
        return remote(at, at, fs.at[(way + 1) // 2, k, c], fr.at[(way + 1) // 2, k, c], {"dp": other})

    def inside(place):
        return jnp.logical_and(place >= 0, place < nz)

    def sends(way, k):
        return jnp.logical_and(inside(z - way * k), inside(z + way))

    def streams(steps):
        return [(way, k, c) for k in range(steps) for c in range(pieces) for way in (1, -1)]

    over = [
        remote(yf.at[cut], yland.at[d, cut], os.at[c], orr.at[c], {"dp": other}) for c, cut in enumerate(cuts)
    ]
    for c in range(pieces):
        for way in (1, -1):
            pl.when(sends(way, 0))(lambda way=way, c=c: along(way, 0, c).start())
        over[c].start()
        if c == 0:
            for copy in x_out:
                copy.start()
    mine = pl.ds(pl.multiple_of(d * block, 128), block)
    keep_x = pltpu.make_async_copy(xf.at[:, mine], xland.at[d], local.at[0])
    keep_y = pltpu.make_async_copy(yf, yland.at[d], local.at[1])
    keep_x.start()
    keep_y.start()

    passed = []
    for k in range(1, nd):
        x_out[k - 1].wait_recv()
        source = lax.rem(d + nd - k, nd)
        for j in range(1, nm):
            copy = remote(
                xland.at[source, part],
                xland.at[source, part],
                ms.at[k - 1, j - 1],
                mr.at[k - 1, j - 1],
                {"mp": lax.rem(m + j, nm)},
            )
            copy.start()
            passed.append(copy)

    def place(mm, dd):
        return pl.ds(pl.multiple_of((mm * nd + dd) * share, 8), share)

    pending = list(x_out) + passed + over

    def behind(k):
        return lax.rem(d + nd - k, nd)

    def reduce(a, k):
        peer = lax.rem(d + k, nd)
        size = share + slab if a == 0 else share
        return remote(
            upart.at[a, peer, pl.ds(0, size)], uland.at[a, d, pl.ds(0, size)],
            us.at[a, k - 1], ur.at[a, k - 1], {"dp": peer},
        )

    def gather(a, k):
        return remote(
            uown.at[a, pl.ds(0, share)], u.at[a, place(m, d)],
            gs.at[a, k - 1], gr.at[a, k - 1], {"dp": lax.rem(d + k, nd)},
        )

    def gather_slab(k):
        return remote(
            uown.at[0, pl.ds(share, slab)], ssf.at[pl.ds(pl.multiple_of(d * slab, 8), slab)],
            ss.at[k - 1], sr.at[k - 1], {"dp": lax.rem(d + k, nd)},
        )

    def hop(a, k, owner, send, recv, to):
        at = u.at[a, place(owner, behind(k))]
        source = uown.at[a, pl.ds(0, share)] if k == 0 and send is not ks else at
        return remote(source, at, send.at[a, k], recv.at[a, k], {"mp": to})

    def to_facing(a, k):
        return hop(a, k, m, ys, yr, facing)

    def to_mate(a, k):
        return hop(a, k, m, cs, cr, mate)

    def on_to_mate(a, k):
        return hop(a, k, facing, ks, kr, mate)

    def sum_start(a, value, extra=None):
        some = exact_left(xb[pl.ds(pl.multiple_of(m * quarter, 8), quarter), :], value)
        upart[a, :, :share] = some.reshape(nd, share, rank)
        if extra is not None:
            upart[a, :, share:] = extra.reshape(nd, slab, rank)
        for k in range(1, nd):
            reduce(a, k).start()

    def sum_own(a):
        size = share + slab if a == 0 else share
        total = upart[a, d, :size]
        for k in range(1, nd):
            reduce(a, k).wait_recv()
            total = total + uland[a, behind(k), :size]
        uown[a, :size] = total
        for k in range(1, nd):
            gather(a, k).start()
        to_facing(a, 0).start()
        to_mate(a, 0).start()
        if a == 0:
            for k in range(1, nd):
                gather_slab(k).start()
            ssf[pl.ds(pl.multiple_of(d * slab, 8), slab)] = total[share:]
        u[a, place(m, d)] = total[:share]

    def sum_pass(a, ks_):
        for k in ks_:
            gather(a, k).wait_recv()
            to_facing(a, k).start()
            to_mate(a, k).start()

    def sum_cross(a, ks_):
        for k in ks_:
            hop(a, k, facing, ys, yr, facing).wait_recv()
            on_to_mate(a, k).start()

    def sum_end(a):
        for k in range(nd):
            to_mate(a, k).wait_recv()
            on_to_mate(a, k).wait_recv()
        if a == 0:
            for k in range(1, nd):
                gather_slab(k).wait_recv()

    def sum_drain(a):
        for k in range(1, nd):
            reduce(a, k).wait_send()
            gather(a, k).wait_send()
            if a == 0:
                gather_slab(k).wait_send()
        for k in range(nd):
            to_facing(a, k).wait_send()
            to_mate(a, k).wait_send()
            on_to_mate(a, k).wait_send()

    bands, half = w.shape[1], w.shape[3]

    def to_core(a, q):
        return remote(ppart.at[a, q, 1 - mc], pland.at[a, q], ps.at[a, q], pr.at[a, q], {"mp": mate})

    def to_chip(a, q):
        return remote(psum.at[a, q], pother.at[a, q], qs.at[a, q], qr.at[a, q], {"mp": facing})

    def back(a, q):
        at = w.at[a, q, mc]
        return remote(at, at, ts.at[a, q], tr.at[a, q], {"mp": mate})

    def images(a, value):
        span = exact_right(value.T, yb[...]).T
        both = halves(span, 1)
        for q in range(bands):
            some = jnp.dot(yb[q * 2 * half : (q + 1) * 2 * half, :], both, preferred_element_type=jnp.float32)
            ppart[a, q] = (folded(some, 1) * (scale * scale)).reshape(2, half, rank)
            to_core(a, q).start()

    def image_chip(a, q):
        to_core(a, q).wait_recv()
        psum[a, q] = ppart[a, q, mc] + pland[a, q]
        to_chip(a, q).start()

    def image_sum(a, q):
        to_chip(a, q).wait_recv()
        w[a, q, mc] = psum[a, q] + pother[a, q]
        back(a, q).start()

    def image_end(a):
        for q in range(bands):
            back(a, q).wait_recv()
        return w[a].reshape(count, rank)

    def image_drain(a):
        for q in range(bands):
            to_core(a, q).wait_send()
            to_chip(a, q).wait_send()
            back(a, q).wait_send()

    def first_sum():
        keep_x.wait()
        for copy in passed:
            copy.wait_recv()
        for s in range(nd):
            xt[:, s * rows : (s + 1) * rows] = xland[s].T.astype(jnp.bfloat16)
            xb[s * rows : (s + 1) * rows, :] = xland[s].astype(jnp.bfloat16)
        sketch = s_ref[...]
        sum_start(0, sketch, gram(sketch, sketch))

    def relay(steps):
        for way, k, c in steps:

            @pl.when(inside(z - way * (k + 1)))
            def _():
                along(way, k, c).wait_recv()
                across(way, k, c).start()

                if k + 1 < nz - 1:

                    @pl.when(inside(z + way))
                    def _():
                        along(way, k + 1, c).start()

    waves = streams(nz - 1)
    per = 2 * pieces
    relay(waves[:per])
    first_sum()
    relay(waves[per : 2 * per])
    sum_own(0)
    relay(waves[2 * per :])
    sum_pass(0, range(1, nd))
    sum_cross(0, range(nd))
    sum_end(0)
    keep_y.wait()
    for copy in over:
        copy.wait_recv()
    for way, k, c in waves:
        pl.when(inside(z - way * (k + 1)))(lambda way=way, k=k, c=c: across(way, k, c).wait())
    for s in range(nd):
        yb[s * rows : (s + 1) * rows, :] = yland[s].astype(jnp.bfloat16)

    square = (rank, rank)
    diagonal = lax.broadcasted_iota(jnp.int32, square, 0) == lax.broadcasted_iota(jnp.int32, square, 1)
    tile = 256 if width % 256 == 0 else width

    def gradient_tile(t, carry):
        cols = pl.ds(pl.multiple_of(t * tile, 128), tile)
        g[:, cols] = scale * jnp.dot(xt[...], yb[:, cols], preferred_element_type=jnp.float32)
        return carry

    images(0, u[0])
    for q in range(bands):
        image_chip(0, q)
    sketch_gram = ssf[...]
    lax.fori_loop(0, width // tile, gradient_tile, 0)
    for q in range(bands):
        image_sum(0, q)
    w0 = image_end(0)
    sum_start(1, exact_left(xt[...], w0))
    mixed0 = DECAY_RATE * times(u[0], sketch_gram)
    proj1 = DECAY_RATE * times(sketch_gram, sketch_gram) + gram(u[0], w0)
    sum_own(1)
    sum_pass(1, range(1, nd))
    sum_cross(1, range(nd))
    sum_end(1)
    kept[...] = mixed0 + u[1]
    images(1, kept[...])
    gram_mat = DECAY_RATE * times(sketch_gram, proj1) + gram(w0, kept[...])
    low = []
    run_with(
        factor_steps(gram_mat, low),
        [functools.partial(image_chip, 1, q) for q in range(bands)]
        + [lambda: None] * 2
        + [functools.partial(image_sum, 1, q) for q in range(bands)],
    )
    low_t = low[0].T
    w1 = times(image_end(1), low_t)
    moved = exact_left(xt[...], w1)
    sum_start(2, moved)
    u1 = times(kept[...], low_t)
    proj1 = times(proj1, low_t)
    rayleigh = DECAY_RATE * gram(proj1, proj1) + gram(u1, w1)
    rayleigh = 0.5 * (rayleigh + rayleigh.T)
    mean_level = jnp.sum(jnp.where(diagonal, rayleigh, 0.0)) / rank
    shifted = rayleigh + jnp.where(diagonal, RIDGE_FRAC * mean_level, 0.0)
    applied = DECAY_RATE * times(s_ref[...], proj1) + moved
    proj2 = DECAY_RATE * times(sketch_gram, proj1) + gram(u[0], w1)
    mixed1 = DECAY_RATE * times(u[0], proj1)
    self_part = DECAY_RATE * gram(proj1, proj2) + mean_level * shifted
    top = []
    run_with(
        factor_steps(shifted, top),
        [lambda: sum_own(2)]
        + [functools.partial(sum_pass, 2, [k]) for k in range(1, nd)]
        + [functools.partial(sum_cross, 2, [k]) for k in range(nd)],
    )
    new_ref[...] = times(applied, top[0].T)
    sum_end(2)
    u2 = mixed1 + u[2]
    bottom = []
    run_with(factor_steps(self_part + gram(w1, u2), bottom), [])
    span = scale * exact_right(u2.T, yb[...])
    mixer = halves(times(times(applied, bottom[0].T), bottom[0]), 1)
    both = halves(span, 0)
    high = jnp.concatenate([both[:rank], both[:rank]], axis=0)
    low = jnp.concatenate([both[rank:], both[rank:]], axis=0)
    for t in range(width // tile):
        cols = slice(t * tile, (t + 1) * tile)
        gone = jnp.dot(mixer, high[:, cols], preferred_element_type=jnp.float32)
        gone = gone + jnp.dot(mixer, low[:, cols], preferred_element_type=jnp.float32)
        pre_ref[:, cols] = (g[:, cols] - gone).astype(jnp.bfloat16)

    for copy in pending:
        copy.wait_send()
    for way, k, c in waves:
        pl.when(sends(way, k))(lambda way=way, k=k, c=c: along(way, k, c).wait_send())
    for a in range(3):
        sum_drain(a)
    for a in range(2):
        image_drain(a)


def whole_fits(tokens, cotangent, sketch):
    nd, nm = lax.axis_size("dp"), lax.axis_size("mp")
    rows, depth = tokens.shape
    width = cotangent.shape[1]
    block, rank = sketch.shape
    need = 4 * rows * (depth + width) + nd * rows * (8 * block + 6 * width) + 4 * block * width
    need += 54 * nd * rows * rank
    return (
        nm == 4
        and nd % 2 == 0
        and nd <= 16
        and rank == 128
        and rows % 128 == 0
        and block % 128 == 0
        and width % 128 == 0
        and rank % (8 * nd) == 0
        and need <= VMEM_BUDGET
    )


def whole(tokens, cotangent, sketch, norm_scale):
    nd, nm = lax.axis_size("dp"), lax.axis_size("mp")
    rows, depth = tokens.shape
    width = cotangent.shape[1]
    block, rank = sketch.shape
    nz = nd // 2
    pieces = 2
    share, slab, count = rows // nm, rank // nd, nd * rows
    bands = 4
    half = count // (2 * bands)
    dma = pltpu.SemaphoreType.DMA
    f32 = jnp.float32
    return pl.pallas_call(
        functools.partial(whole_kernel, nd, nm, pieces, norm_scale),
        out_shape=(
            jax.ShapeDtypeStruct((block, width), jnp.bfloat16),
            jax.ShapeDtypeStruct((block, rank), f32),
        ),
        in_specs=[pl.BlockSpec(memory_space=VMEM)] * 3,
        out_specs=(pl.BlockSpec(memory_space=VMEM),) * 2,
        scratch_shapes=[
            pltpu.VMEM((rows, depth), f32),
            pltpu.VMEM((rows, width), f32),
            pltpu.VMEM((nd, rows, block), f32),
            pltpu.VMEM((nd, rows, width), f32),
            pltpu.VMEM((block, count), jnp.bfloat16),
            pltpu.VMEM((count, block), jnp.bfloat16),
            pltpu.VMEM((count, width), jnp.bfloat16),
            pltpu.VMEM((block, width), f32),
            pltpu.VMEM((3, nd, share + slab, rank), f32),
            pltpu.VMEM((3, nd, share + slab, rank), f32),
            pltpu.VMEM((3, share + slab, rank), f32),
            pltpu.VMEM((3, count, rank), f32),
            pltpu.VMEM((count, rank), f32),
            pltpu.VMEM((rank, rank), f32),
            pltpu.VMEM((2, bands, 2, half, rank), f32),
            pltpu.VMEM((2, bands, half, rank), f32),
            pltpu.VMEM((2, bands, half, rank), f32),
            pltpu.VMEM((2, bands, half, rank), f32),
            pltpu.VMEM((2, bands, 2, half, rank), f32),
            dma((2,)),
            dma((nd - 1,)),
            dma((nd - 1,)),
            dma((nd - 1, nm - 1)),
            dma((nd - 1, nm - 1)),
            dma((2, nz - 1, pieces)),
            dma((2, nz - 1, pieces)),
            dma((2, nz - 1, pieces)),
            dma((2, nz - 1, pieces)),
            dma((pieces,)),
            dma((pieces,)),
        ]
        + [dma((3, nd - 1))] * 4
        + [dma((nd - 1,))] * 2
        + [dma((3, nd))] * 6
        + [dma((2, bands))] * 6,
        compiler_params=pltpu.CompilerParams(
            collective_id=6, has_side_effects=True, vmem_limit_bytes=60 * 2**20
        ),
        name="whole",
    )(tokens, cotangent, sketch)


def shards(tokens, cotangent, sketch):
    norm_scale = 1.0 / math.sqrt(tokens.shape[0] * lax.axis_size("dp"))
    if whole_fits(tokens, cotangent, sketch):
        return whole(tokens, cotangent, sketch, norm_scale)
    gradient = gradient_block(tokens, cotangent, norm_scale)

    grad_proj, sketch_proj = all_sum(
        (product(gradient, sketch, TN), product(sketch, sketch, TN)), "dp", 1
    )
    (summed,) = all_sum((product(gradient, grad_proj),), "mp", 2)
    previous = DECAY_RATE * product(sketch, sketch_proj) + summed
    grad_image, sketch_image, gram_mat = all_sum(
        (
            product(gradient, previous, TN),
            product(sketch, previous, TN),
            product(previous, previous, TN),
        ),
        "dp",
        3,
    )
    summed, low_inv = all_sum((product(gradient, grad_image),), "mp", 4, gram_mat)
    applied = product(DECAY_RATE * product(sketch, sketch_image) + summed, low_inv, NT)
    image_grad, cross_prev, self_image = all_sum(
        (
            product(gradient, applied, TN),
            product(previous, applied, TN),
            product(applied, applied, TN),
        ),
        "dp",
        5,
    )
    new_inv, mixer = small_call(finish_kernel, 2, "finish", low_inv, cross_prev, self_image)
    new_sketch = product(applied, new_inv, NT)
    precond = gradient - product(product(new_sketch, mixer), image_grad, NT)
    return (precond.astype(jnp.bfloat16), new_sketch)


def solution(mesh):
    in_specs = (P("dp", None), P("dp", "mp"), P("dp", None))
    out_specs = (P("dp", "mp"), P("dp", None))
    return jax.shard_map(shards, mesh=mesh, in_specs=in_specs, out_specs=out_specs, check_vma=False)
```

profile of v0, /device:TPU:1, one launch (start us, length us, event | category | flops | bytes accessed | tf_op | source)
XLA Modules:
  0.0 152.1 jit_solution(14293090878070241564)
XLA Ops:
  0.6 148.5 %whole.1 = (bf16[512,1024]{1,0:T(8,128)(2,1)}, f32[512,128]{1,0:T(8,128)}) custom-call(bf16[128,4096]{1,0:T(8,128)(2,1)} %tok_ref.1, bf16[128,1024]{1,0:T(8,128)(2,1)} %cot_ref.1, f32[512,128]{1,0:T(8,128)} %s_ref.1), custom_call_target="tpu_custom_call" | custom-call | tf_op jit(solution)/shard_map/whole/pallas_call | solution.py:810
  149.1 0.0 copy-start
  149.1 2.3 %copy.7 = bf16[512,1024]{1,0:T(8,128)(2,1)} copy(bf16[512,1024]{1,0:T(8,128)(2,1)} %get-tuple-element.4) | data formatting | bytes 2097152
  151.4 0.0 copy-done
  151.4 0.7 copy.8
Async XLA Ops:
  149.1 2.3 %copy-start = (f32[512,128]{1,0:T(8,128)S(1)}, f32[512,128]{1,0:T(8,128)}, u32[]{:S(2)}) copy-start(f32[512,128]{1,0:T(8,128)} %get-tuple-element.5) | copy-start | bytes 786436
where the time goes:
time: 152 us
  Pallas kernels  148 us (97%)
  local copies, waits for them, and re-layouts  3.01 us (2%)
    pallas_call x1, Pallas kernels, whole(): pl.pallas_call(functools.partial(whole_kernel, nd, nm, pieces, norm_scale...  148 us

commit v1 on v0

--- a/solution.py
+++ b/solution.py
@@ -376,37 +376,47 @@
     return folded(folded(full, 0), 1)
 
 
+def spread(value, column):
+    return jnp.take_along_axis(value, jnp.full(value.shape, column, jnp.int32), axis=1)
+
+
 def factor_steps(matrix, result):
     n = matrix.shape[0]
+    tile = (8, n)
     start = jnp.where(
         lax.broadcasted_iota(jnp.int32, (n, n), 0) == lax.broadcasted_iota(jnp.int32, (n, n), 1), 1.0, 0.0
     ).astype(jnp.float32)
     left = [matrix[8 * i : 8 * i + 8] for i in range(n // 8)]
     right = [start[8 * i : 8 * i + 8] for i in range(n // 8)]
-    row_of = lax.broadcasted_iota(jnp.int32, (8, 1), 0)
+    row_of = lax.broadcasted_iota(jnp.int32, tile, 0)
     rows = []
-    for j in range(0, n, 2):
-        t, s = divmod(j, 8)
-        a0, a1 = left[t][s : s + 1], left[t][s + 1 : s + 2]
-        b0, b1 = right[t][s : s + 1], right[t][s + 1 : s + 2]
-        pivot, side, corner = a0[:, j : j + 1], a0[:, j + 1 : j + 2], a1[:, j + 1 : j + 2]
-        inv0 = 1.0 / pivot
-        factor = side * inv0
-        a1, b1 = a1 - factor * a0, b1 - factor * b0
-        second = corner - factor * side
-        inv1 = 1.0 / second
-        rows += [b0 * lax.rsqrt(pivot), b1 * lax.rsqrt(second)]
-        a0, b0, a1, b1 = a0 * inv0, b0 * inv0, a1 * inv1, b1 * inv1
-        for i in range(t, n // 8):
-            c0, c1 = left[i][:, j : j + 1], left[i][:, j + 1 : j + 2]
-            c1 = c1 - factor * c0
-            if i == t:
-                c0 = jnp.where(row_of > s + 1, c0, 0.0)
-                c1 = jnp.where(row_of > s + 1, c1, 0.0)
-            left[i] = left[i] - c0 * a0 - c1 * a1
-            right[i] = right[i] - c0 * b0 - c1 * b1
-        if s == 6:
-            yield
+
+    def row(value, k):
+        return jnp.broadcast_to(value[k : k + 1], tile)
+
+    for t in range(n // 8):
+        above, inverse = left[t], right[t]
+        columns = [spread(above, 8 * t + k) for k in range(8)]
+        done = []
+        for k in range(8):
+            pivot = row(columns[k], k)
+            scale = 1.0 / pivot
+            a, b = row(above, k) * scale, row(inverse, k) * scale
+            rows.append((row(inverse, k) * lax.rsqrt(pivot))[:1])
+            weights = [row(columns[q], k) * scale for q in range(k + 1, 8)]
+            done.append((a, b, weights))
+            c = jnp.where(row_of > k, columns[k], 0.0)
+            above, inverse = above - c * a, inverse - c * b
+            for q in range(k + 1, 8):
+                columns[q] = columns[q] - c * weights[q - k - 1]
+        for i in range(t + 1, n // 8):
+            columns = [spread(left[i], 8 * t + k) for k in range(8)]
+            for k, (a, b, weights) in enumerate(done):
+                c = columns[k]
+                left[i], right[i] = left[i] - c * a, right[i] - c * b
+                for q in range(k + 1, 8):
+                    columns[q] = columns[q] - c * weights[q - k - 1]
+        yield
     result.append(jnp.concatenate(rows, axis=0))
 
 
@@ -419,12 +429,12 @@
         action()
 
 
-def whole_kernel(nd, nm, pieces, scale, tok_ref, cot_ref, s_ref, pre_ref, new_ref, *refs):
+def whole_kernel(nd, nm, pieces, scale, tok_ref, cot_ref, sketch_ref, g, mixer_ref, span_ref, new_ref, *refs):
     (
-        xf, yf, xland, yland, xt, xb, yb, g, upart, uland, uown, u, kept, ssf,
+        tok, cot, s_ref, got, xf, yf, xland, yland, xt, xb, yb, upart, uland, uown, u, kept, ssf, wpart, wland, wsum,
         ppart, pland, psum, pother, w,
         local, xs, xr, ms, mr, zs, zr, fs, fr, os, orr,
-        us, ur, gs, gr, ss, sr, ys, yr, cs, cr, ks, kr,
+        twins, twinr, us, ur, gs, gr, ss, sr, vs, vr, hs, hr, ys, yr, cs, cr, ks, kr,
         ps, pr, qs, qr, ts, tr,
     ) = refs
     d, m = lax.axis_index("dp"), lax.axis_index("mp")
@@ -446,8 +456,16 @@
         pl.semaphore_signal(barrier, inc=1, device_id={"dp": lax.rem(d + k, nd)}, device_id_type=MESH)
     for k in range(1, nm):
         pl.semaphore_signal(barrier, inc=1, device_id={"mp": lax.rem(m + k, nm)}, device_id_type=MESH)
-    yf[...] = cot_ref[...].astype(jnp.float32)
-    xf[...] = tok_ref[...].astype(jnp.float32)
+    fetch = [
+        pltpu.make_async_copy(source, to, got.at[n])
+        for n, (source, to) in enumerate([(tok_ref, tok), (cot_ref, cot), (sketch_ref, s_ref)])
+    ]
+    for copy in fetch:
+        copy.start()
+    for copy in fetch:
+        copy.wait()
+    xf[...] = tok[...].astype(jnp.float32)
+    yf[...] = cot[...].astype(jnp.float32)
     pl.semaphore_wait(barrier, nd + nm - 2)
 
     part = pl.ds(pl.multiple_of(m * share, 8), share)
@@ -486,31 +504,27 @@
     over = [
         remote(yf.at[cut], yland.at[d, cut], os.at[c], orr.at[c], {"dp": other}) for c, cut in enumerate(cuts)
     ]
+    for copy in x_out:
+        copy.start()
     for c in range(pieces):
         for way in (1, -1):
             pl.when(sends(way, 0))(lambda way=way, c=c: along(way, 0, c).start())
         over[c].start()
-        if c == 0:
-            for copy in x_out:
-                copy.start()
     mine = pl.ds(pl.multiple_of(d * block, 128), block)
     keep_x = pltpu.make_async_copy(xf.at[:, mine], xland.at[d], local.at[0])
     keep_y = pltpu.make_async_copy(yf, yland.at[d], local.at[1])
     keep_x.start()
     keep_y.start()
 
+    def share_of(k, owner, way, to):
+        at = xland.at[lax.rem(d + nd - k, nd), pl.ds(pl.multiple_of(owner * share, 8), share)]
+        return remote(at, at, ms.at[k - 1, way], mr.at[k - 1, way], {"mp": to})
+
     passed = []
     for k in range(1, nd):
         x_out[k - 1].wait_recv()
-        source = lax.rem(d + nd - k, nd)
-        for j in range(1, nm):
-            copy = remote(
-                xland.at[source, part],
-                xland.at[source, part],
-                ms.at[k - 1, j - 1],
-                mr.at[k - 1, j - 1],
-                {"mp": lax.rem(m + j, nm)},
-            )
+        for way, to in ((0, facing), (1, mate)):
+            copy = share_of(k, m, way, to)
             copy.start()
             passed.append(copy)
 
@@ -518,6 +532,13 @@
         return pl.ds(pl.multiple_of((mm * nd + dd) * share, 8), share)
 
     pending = list(x_out) + passed + over
+
+    def pass_on():
+        for k in range(1, nd):
+            share_of(k, facing, 0, facing).wait_recv()
+            copy = share_of(k, facing, 2, mate)
+            copy.start()
+            pending.append(copy)
 
     def behind(k):
         return lax.rem(d + nd - k, nd)
@@ -536,11 +557,16 @@
             gs.at[a, k - 1], gr.at[a, k - 1], {"dp": lax.rem(d + k, nd)},
         )
 
-    def gather_slab(k):
+    def gather_slab(a, k):
         return remote(
-            uown.at[0, pl.ds(share, slab)], ssf.at[pl.ds(pl.multiple_of(d * slab, 8), slab)],
+            uown.at[a, pl.ds(share, slab)], ssf.at[pl.ds(pl.multiple_of(d * slab, 8), slab)],
             ss.at[k - 1], sr.at[k - 1], {"dp": lax.rem(d + k, nd)},
         )
+
+    def slab_end(a):
+        for k in range(1, nd):
+            gather_slab(a, k).wait_recv()
+        return ssf[...]
 
     def hop(a, k, owner, send, recv, to):
         at = u.at[a, place(owner, behind(k))]
@@ -571,14 +597,14 @@
             reduce(a, k).wait_recv()
             total = total + uland[a, behind(k), :size]
         uown[a, :size] = total
+        if a == 0:
+            for k in range(1, nd):
+                gather_slab(a, k).start()
+            ssf[pl.ds(pl.multiple_of(d * slab, 8), slab)] = total[share:]
         for k in range(1, nd):
             gather(a, k).start()
         to_facing(a, 0).start()
         to_mate(a, 0).start()
-        if a == 0:
-            for k in range(1, nd):
-                gather_slab(k).start()
-            ssf[pl.ds(pl.multiple_of(d * slab, 8), slab)] = total[share:]
         u[a, place(m, d)] = total[:share]
 
     def sum_pass(a, ks_):
@@ -596,20 +622,60 @@
         for k in range(nd):
             to_mate(a, k).wait_recv()
             on_to_mate(a, k).wait_recv()
-        if a == 0:
-            for k in range(1, nd):
-                gather_slab(k).wait_recv()
 
     def sum_drain(a):
         for k in range(1, nd):
             reduce(a, k).wait_send()
             gather(a, k).wait_send()
             if a == 0:
-                gather_slab(k).wait_send()
+                gather_slab(a, k).wait_send()
         for k in range(nd):
             to_facing(a, k).wait_send()
             to_mate(a, k).wait_send()
             on_to_mate(a, k).wait_send()
+
+    band = wland.shape[1]
+
+    def band_of(owner):
+        return pl.ds(pl.multiple_of(owner * band, 8), band)
+
+    def part_out(k):
+        return remote(wpart.at[band_of(m)], wland.at[d], vs.at[k - 1], vr.at[k - 1], {"dp": lax.rem(d + k, nd)})
+
+    def part_share(n, owner, to):
+        at = wsum.at[band_of(owner)]
+        return remote(at, at, hs.at[n], hr.at[n], {"mp": to})
+
+    def small_start(value):
+        wpart[...] = value
+        for k in range(1, nd):
+            part_out(k).start()
+        wland[d] = wpart[band_of(m)]
+
+    def small_sum():
+        for k in range(1, nd):
+            part_out(k).wait_recv()
+        total = wland[0]
+        for n in range(1, nd):
+            total = total + wland[n]
+        wsum[band_of(m)] = total
+        part_share(0, m, facing).start()
+        part_share(1, m, mate).start()
+
+    def small_pass():
+        part_share(0, facing, facing).wait_recv()
+        part_share(2, facing, mate).start()
+
+    def small_end():
+        part_share(1, m, mate).wait_recv()
+        part_share(2, m, mate).wait_recv()
+        return wsum[...]
+
+    def small_drain():
+        for k in range(1, nd):
+            part_out(k).wait_send()
+        for n in range(3):
+            part_share(n, m, mate).wait_send()
 
     bands, half = w.shape[1], w.shape[3]
 
@@ -654,21 +720,36 @@
 
     def first_sum():
         keep_x.wait()
-        for copy in passed:
-            copy.wait_recv()
+        for k in range(1, nd):
+            share_of(k, m, 1, mate).wait_recv()
+            share_of(k, m, 2, mate).wait_recv()
         for s in range(nd):
             xt[:, s * rows : (s + 1) * rows] = xland[s].T.astype(jnp.bfloat16)
             xb[s * rows : (s + 1) * rows, :] = xland[s].astype(jnp.bfloat16)
         sketch = s_ref[...]
         sum_start(0, sketch, gram(sketch, sketch))
 
+    def twin(way):
+        at = yland.at[other, cuts[0]]
+        n = (way + 1) // 2
+        return remote(at, at, twins.at[n], twinr.at[n], {"dp": 2 * (z + way) + x})
+
+    def by_twin(k, c):
+        return k == 0 and c == 0
+
+    def start_twins():
+        over[0].wait_recv()
+        for way in (1, -1):
+            pl.when(inside(z + way))(lambda way=way: twin(way).start())
+
     def relay(steps):
         for way, k, c in steps:
 
             @pl.when(inside(z - way * (k + 1)))
             def _():
                 along(way, k, c).wait_recv()
-                across(way, k, c).start()
+                if not by_twin(k, c):
+                    across(way, k, c).start()
 
                 if k + 1 < nz - 1:
 
@@ -677,20 +758,28 @@
                         along(way, k + 1, c).start()
 
     waves = streams(nz - 1)
-    per = 2 * pieces
-    relay(waves[:per])
-    first_sum()
-    relay(waves[per : 2 * per])
-    sum_own(0)
-    relay(waves[2 * per :])
-    sum_pass(0, range(1, nd))
-    sum_cross(0, range(nd))
+    plan = {
+        (0, 0): pass_on,
+        (0, 1): first_sum,
+        (1, 2): lambda: sum_own(0),
+        (2, 2): lambda: sum_pass(0, range(1, nd)),
+        (2, 3): lambda: sum_cross(0, range(nd)),
+    }
+    start_twins()
+    for k in range(nz - 1):
+        for c in range(pieces):
+            relay([(way, k, c) for way in (1, -1)])
+            plan.get((k, c), lambda: None)()
     sum_end(0)
+    sketch_gram = slab_end(0)
+    mixed0 = DECAY_RATE * times(u[0], sketch_gram)
+    square_gram = DECAY_RATE * times(sketch_gram, sketch_gram)
     keep_y.wait()
-    for copy in over:
+    for copy in over[1:]:
         copy.wait_recv()
     for way, k, c in waves:
-        pl.when(inside(z - way * (k + 1)))(lambda way=way, k=k, c=c: across(way, k, c).wait())
+        last = twin(way).wait_recv if by_twin(k, c) else across(way, k, c).wait
+        pl.when(inside(z - way * (k + 1)))(lambda last=last: last())
     for s in range(nd):
         yb[s * rows : (s + 1) * rows, :] = yland[s].astype(jnp.bfloat16)
 
@@ -706,14 +795,12 @@
     images(0, u[0])
     for q in range(bands):
         image_chip(0, q)
-    sketch_gram = ssf[...]
     lax.fori_loop(0, width // tile, gradient_tile, 0)
     for q in range(bands):
         image_sum(0, q)
     w0 = image_end(0)
     sum_start(1, exact_left(xt[...], w0))
-    mixed0 = DECAY_RATE * times(u[0], sketch_gram)
-    proj1 = DECAY_RATE * times(sketch_gram, sketch_gram) + gram(u[0], w0)
+    proj1 = square_gram + gram(u[0], w0)
     sum_own(1)
     sum_pass(1, range(1, nd))
     sum_cross(1, range(nd))
@@ -724,55 +811,85 @@
     low = []
     run_with(
         factor_steps(gram_mat, low),
-        [functools.partial(image_chip, 1, q) for q in range(bands)]
-        + [lambda: None] * 2
+        [lambda: None] * 3
+        + [functools.partial(image_chip, 1, q) for q in range(bands)]
+        + [lambda: None] * 4
         + [functools.partial(image_sum, 1, q) for q in range(bands)],
     )
     low_t = low[0].T
     w1 = times(image_end(1), low_t)
     moved = exact_left(xt[...], w1)
+    proj1 = times(proj1, low_t)
+    applied = DECAY_RATE * times(s_ref[...], proj1) + moved
+    small_start(gram(applied, applied))
     sum_start(2, moved)
     u1 = times(kept[...], low_t)
-    proj1 = times(proj1, low_t)
     rayleigh = DECAY_RATE * gram(proj1, proj1) + gram(u1, w1)
     rayleigh = 0.5 * (rayleigh + rayleigh.T)
     mean_level = jnp.sum(jnp.where(diagonal, rayleigh, 0.0)) / rank
     shifted = rayleigh + jnp.where(diagonal, RIDGE_FRAC * mean_level, 0.0)
-    applied = DECAY_RATE * times(s_ref[...], proj1) + moved
-    proj2 = DECAY_RATE * times(sketch_gram, proj1) + gram(u[0], w1)
-    mixed1 = DECAY_RATE * times(u[0], proj1)
-    self_part = DECAY_RATE * gram(proj1, proj2) + mean_level * shifted
     top = []
     run_with(
         factor_steps(shifted, top),
-        [lambda: sum_own(2)]
-        + [functools.partial(sum_pass, 2, [k]) for k in range(1, nd)]
-        + [functools.partial(sum_cross, 2, [k]) for k in range(nd)],
+        [lambda: None] * 9 + [small_sum, lambda: sum_own(2), lambda: None, lambda: None, lambda: None, small_pass],
+    )
+    inner = small_end() + mean_level * shifted
+    bottom = []
+    run_with(
+        factor_steps(inner, bottom),
+        [lambda: None] * 5
+        + [functools.partial(sum_pass, 2, range(1, 4)), functools.partial(sum_pass, 2, range(4, nd))]
+        + [lambda: None] * 2
+        + [functools.partial(sum_cross, 2, range(4)), functools.partial(sum_cross, 2, range(4, nd))],
     )
     new_ref[...] = times(applied, top[0].T)
+    mixed1 = DECAY_RATE * times(u[0], proj1)
+    mixer = halves(times(times(applied, bottom[0].T), bottom[0]), 1)
     sum_end(2)
     u2 = mixed1 + u[2]
-    bottom = []
-    run_with(factor_steps(self_part + gram(w1, u2), bottom), [])
     span = scale * exact_right(u2.T, yb[...])
-    mixer = halves(times(times(applied, bottom[0].T), bottom[0]), 1)
-    both = halves(span, 0)
-    high = jnp.concatenate([both[:rank], both[:rank]], axis=0)
-    low = jnp.concatenate([both[rank:], both[rank:]], axis=0)
-    for t in range(width // tile):
-        cols = slice(t * tile, (t + 1) * tile)
-        gone = jnp.dot(mixer, high[:, cols], preferred_element_type=jnp.float32)
-        gone = gone + jnp.dot(mixer, low[:, cols], preferred_element_type=jnp.float32)
-        pre_ref[:, cols] = (g[:, cols] - gone).astype(jnp.bfloat16)
+    span_ref[...] = span
+    mixer_ref[...] = mixer
 
     for copy in pending:
         copy.wait_send()
     for way, k, c in waves:
         pl.when(sends(way, k))(lambda way=way, k=k, c=c: along(way, k, c).wait_send())
+    for way in (1, -1):
+        pl.when(inside(z + way))(lambda way=way: twin(way).wait_send())
     for a in range(3):
         sum_drain(a)
     for a in range(2):
         image_drain(a)
+    small_drain()
+
+
+def last_kernel(g_ref, mixer_ref, span_ref, new_in_ref, pre_ref, new_ref):
+    new_ref[...] = new_in_ref[...]
+    rank, width = span_ref.shape
+    mixer = mixer_ref[...]
+    tile = 256 if width % 256 == 0 else width
+    for t in range(width // tile):
+        cols = slice(t * tile, (t + 1) * tile)
+        both = halves(span_ref[:, cols], 0)
+        high = jnp.concatenate([both[:rank], both[:rank]], axis=0)
+        low = jnp.concatenate([both[rank:], both[rank:]], axis=0)
+        gone = jnp.dot(mixer, high, preferred_element_type=jnp.float32)
+        gone = gone + jnp.dot(mixer, low, preferred_element_type=jnp.float32)
+        pre_ref[:, cols] = (g_ref[:, cols] - gone).astype(jnp.bfloat16)
+
+
+def last(gradient, mixer, span, new_sketch):
+    return pl.pallas_call(
+        last_kernel,
+        out_shape=(
+            jax.ShapeDtypeStruct(gradient.shape, jnp.bfloat16),
+            jax.ShapeDtypeStruct(new_sketch.shape, jnp.float32),
+        ),
+        in_specs=[pl.BlockSpec(memory_space=VMEM)] * 4,
+        out_specs=(pl.BlockSpec(memory_space=VMEM),) * 2,
+        name="last",
+    )(gradient, mixer, span, new_sketch)
 
 
 def whole_fits(tokens, cotangent, sketch):
@@ -780,7 +897,7 @@
     rows, depth = tokens.shape
     width = cotangent.shape[1]
     block, rank = sketch.shape
-    need = 4 * rows * (depth + width) + nd * rows * (8 * block + 6 * width) + 4 * block * width
+    need = 6 * rows * (depth + width) + nd * rows * (8 * block + 6 * width) + 4 * block * width
     need += 54 * nd * rows * rank
     return (
         nm == 4
@@ -788,6 +905,7 @@
         and nd <= 16
         and rank == 128
         and rows % 128 == 0
+        and nd >= 8
         and block % 128 == 0
         and width % 128 == 0
         and rank % (8 * nd) == 0
@@ -801,8 +919,8 @@
     width = cotangent.shape[1]
     block, rank = sketch.shape
     nz = nd // 2
-    pieces = 2
-    share, slab, count = rows // nm, rank // nd, nd * rows
+    pieces = 4
+    share, slab, band, count = rows // nm, rank // nd, rank // nm, nd * rows
     bands = 4
     half = count // (2 * bands)
     dma = pltpu.SemaphoreType.DMA
@@ -810,12 +928,18 @@
     return pl.pallas_call(
         functools.partial(whole_kernel, nd, nm, pieces, norm_scale),
         out_shape=(
-            jax.ShapeDtypeStruct((block, width), jnp.bfloat16),
+            jax.ShapeDtypeStruct((block, width), f32),
+            jax.ShapeDtypeStruct((block, 2 * rank), jnp.bfloat16),
+            jax.ShapeDtypeStruct((rank, width), f32),
             jax.ShapeDtypeStruct((block, rank), f32),
         ),
-        in_specs=[pl.BlockSpec(memory_space=VMEM)] * 3,
-        out_specs=(pl.BlockSpec(memory_space=VMEM),) * 2,
+        in_specs=[pl.BlockSpec(memory_space=pl.ANY)] * 3,
+        out_specs=(pl.BlockSpec(memory_space=VMEM),) * 4,
         scratch_shapes=[
+            pltpu.VMEM((rows, depth), jnp.bfloat16),
+            pltpu.VMEM((rows, width), jnp.bfloat16),
+            pltpu.VMEM((block, rank), f32),
+            dma((3,)),
             pltpu.VMEM((rows, depth), f32),
             pltpu.VMEM((rows, width), f32),
             pltpu.VMEM((nd, rows, block), f32),
@@ -823,12 +947,14 @@
             pltpu.VMEM((block, count), jnp.bfloat16),
             pltpu.VMEM((count, block), jnp.bfloat16),
             pltpu.VMEM((count, width), jnp.bfloat16),
-            pltpu.VMEM((block, width), f32),
             pltpu.VMEM((3, nd, share + slab, rank), f32),
             pltpu.VMEM((3, nd, share + slab, rank), f32),
             pltpu.VMEM((3, share + slab, rank), f32),
             pltpu.VMEM((3, count, rank), f32),
             pltpu.VMEM((count, rank), f32),
+            pltpu.VMEM((rank, rank), f32),
+            pltpu.VMEM((rank, rank), f32),
+            pltpu.VMEM((nd, band, rank), f32),
             pltpu.VMEM((rank, rank), f32),
             pltpu.VMEM((2, bands, 2, half, rank), f32),
             pltpu.VMEM((2, bands, half, rank), f32),
@@ -846,9 +972,13 @@
             dma((2, nz - 1, pieces)),
             dma((pieces,)),
             dma((pieces,)),
+            dma((2,)),
+            dma((2,)),
         ]
         + [dma((3, nd - 1))] * 4
         + [dma((nd - 1,))] * 2
+        + [dma((nd - 1,))] * 2
+        + [dma((3,))] * 2
         + [dma((3, nd))] * 6
         + [dma((2, bands))] * 6,
         compiler_params=pltpu.CompilerParams(
@@ -861,7 +991,7 @@
 def shards(tokens, cotangent, sketch):
     norm_scale = 1.0 / math.sqrt(tokens.shape[0] * lax.axis_size("dp"))
     if whole_fits(tokens, cotangent, sketch):
-        return whole(tokens, cotangent, sketch, norm_scale)
+        return last(*whole(tokens, cotangent, sketch, norm_scale))
     gradient = gradient_block(tokens, cotangent, norm_scale)
 
     grad_proj, sketch_proj = all_sum(

time: 152 us -> 131 us (0.86)
  Pallas kernels: 148 us -> 130 us
  local copies, waits for them, and re-layouts: 3.01 us -> 0 us
    pallas_call x1, Pallas kernels: 148 us -> 126 us  [whole(): pl.pallas_call(functools.partial(whole_kernel, nd, nm, pieces, norm_scale...]
    pallas_call x0 -> x1, Pallas kernels: none -> 3.55 us  [last(): pl.pallas_call(last_kernel, out_shape=(jax.ShapeDtypeStruct(gradient.shap...]
    unnamed x4 -> x0, local copies, waits for them, and re-layouts: 3.01 us -> none
where the time goes in v1:
time: 131 us
  Pallas kernels  130 us (99%)
    pallas_call x1, Pallas kernels, whole(): pl.pallas_call(functools.partial(whole_kernel, nd, nm, pieces, norm_scale...  126 us
    pallas_call x1, Pallas kernels, last(): pl.pallas_call(last_kernel, out_shape=(jax.ShapeDtypeStruct(gradient.shap...  3.55 us

profile of v1, /device:TPU:1, one launch (start us, length us, event | category | flops | bytes accessed | tf_op | source)
XLA Modules:
  0.0 130.5 jit_solution(6301589763319990918)
XLA Ops:
  0.6 126.3 %whole.1 = (f32[512,1024]{1,0:T(8,128)}, bf16[512,256]{1,0:T(8,128)(2,1)}, f32[128,1024]{1,0:T(8,128)}, f32[512,128]{1,0:T(8,128)}) custom-call(bf16[128,4096]{1,0:T(8,128)(2,1)} %tok_ref.1, bf16[128,1024]{1,0:T(8,128)(2,1)} %cot_ref.1, f32[512,128]{1,0:T(8,128)} %sketch_ref.1), custom_call_target="tpu_custom_call" | custom-call | tf_op jit(solution)/shard_map/whole/pallas_call | solution.py:928
  127.0 3.6 %last.1 = (bf16[512,1024]{1,0:T(8,128)(2,1)}, f32[512,128]{1,0:T(8,128)}) custom-call(f32[512,1024]{1,0:T(8,128)} %get-tuple-element.6.g_ref, bf16[512,256]{1,0:T(8,128)(2,1)} %get-tuple-element.7.mixer_ref, f32[128,1024]{1,0:T(8,128)} %get-tuple-element.8.span_ref, f32[512,128]{1,0:T(8,128)} %get-tuple-element.9.new_in_ref), custom_call_target="tpu_custom_call" | custom-call | tf_op jit(solution)/shard_map/last/pallas_call | solution.py:883
